TPU v7x, 32 devices: a whole 2x2x4 slice. The times are simulated.
32 devices in a mesh: gx: 2 (over y), gy: 4 (over x, core), gz: 4 (over z).
Axes of the slice: x: 2, y: 2, z: 4, core: 2. Of those that a mesh axis runs over, the one named last changes fastest.
Arguments:
- velocity: float32 [32, 64, 3, 512], P('gx', 'gy', None, 'gz'), may hold values from -6 to 6
- marker_pos: float32 [2048, 3, 256], P(('gx', 'gy', 'gz')), may hold values from -130 to 256
- marker_force: float32 [2048, 3, 256], P(('gx', 'gy', 'gz')), may hold values from -6 to 6
- intersect: int32 [2048, 27], P(('gx', 'gy', 'gz')), may hold values from 0 to 1, as said below
- tiles: int32 [2048, 27, 16], P(('gx', 'gy', 'gz')), may hold values from 0 to 255, as said below
Outputs:
- velocity_out: float32 [32, 64, 3, 512], P('gx', 'gy', None, 'gz')
- marker_velocity: float32 [2048, 3, 256], P(('gx', 'gy', 'gz'))
Inputs may be any that keep to these rules, and one draw needn't show every extreme that they name: `intersect`: column 13 is always 1. Of one owner's bubbles at most 16 have a 1 in any other column; on every draw some owner has exactly 16 in some column, and some device is intersected by exactly 16 bubbles of its neighbour at each of the 26 other offsets. tiles[b, q, j] is a tile of the device at offset q from b's owner, numbered ix * 16 + iy for the line of cells (ix, iy); entries of columns where intersect is 0 are not used.
All inputs are finite; a program needn't handle non-finite values.
Results may differ from a plain program's by a relative error of at most 0.0049.
Values sent between devices are 32-bit elements; how exact they have to be, the bound alone decides.
A program may use at most 128 MiB of HBM per device.

v0:
```python
import functools

import jax
import jax.numpy as jnp
import numpy as np
from jax import lax
from jax.experimental import pallas as pl
from jax.experimental.pallas import tpu as pltpu
from jax.sharding import PartitionSpec as P

CAP = 16
STEPS = (CAP // 4, CAP // 2, CAP)
VMEM_LIMIT = 20 << 20

spread_width = 0.5
viscous = 0.1
scale = float(np.sqrt(spread_width * np.log2(np.e)))

VMEM = pl.BlockSpec(memory_space=pltpu.VMEM)
SMEM = pl.BlockSpec(memory_space=pltpu.SMEM)


def shifted(value, axis, step):
    count = lax.axis_size(axis)
    return lax.ppermute(value, axis, [(i, (i + step) % count) for i in range(count)])


def message(marker_pos, marker_force, intersect, tiles):
    bubbles, _, markers = marker_pos.shape
    touched = tiles.shape[2]
    own_lists = bubbles // CAP
    ranking = jnp.cumsum(intersect, axis=0) - 1
    slot = jnp.arange(CAP, dtype=jnp.int32)
    matches = (ranking.T[:, None, :] == slot[None, :, None]) & (intersect.T[:, None, :] == 1)
    bubble = jnp.arange(bubbles, dtype=jnp.int32)
    picked = jnp.sum(jnp.where(matches, bubble[None, None, :], 0), axis=2)
    counts = jnp.minimum(jnp.sum(intersect, axis=0), CAP)
    used = slot[None, :] < counts[:, None]
    listed = jnp.einsum(
        "qsb,bqj->qsj",
        matches.astype(jnp.bfloat16),
        tiles.astype(jnp.bfloat16),
        preferred_element_type=jnp.float32,
    )
    listed = jnp.where(used[:, :, None], listed, -1.0).reshape(27, CAP * touched)
    own_tiles = tiles[:, 13, :].astype(jnp.float32).reshape(own_lists, CAP * touched)
    listed = jnp.concatenate([listed[:13], own_tiles[:1], listed[14:], own_tiles[1:]], axis=0)
    own_picks = bubble.reshape(own_lists, CAP)
    picks = jnp.concatenate([picked[:13], own_picks[:1], picked[14:], own_picks[1:]], axis=0)
    counts = jnp.concatenate(
        [counts[:13], jnp.full((1,), CAP), counts[14:], jnp.full((own_lists - 1,), CAP)]
    )
    lists = jnp.concatenate([picks.reshape(-1), counts]).astype(jnp.float32)
    lists = jnp.pad(lists, (0, -lists.shape[0] % markers)).reshape(-1, markers)
    packed = jnp.concatenate(
        [
            marker_pos.transpose(1, 0, 2).reshape(-1, markers),
            marker_force.transpose(1, 0, 2).reshape(-1, markers),
            listed,
            lists,
        ],
        axis=0,
    )
    return jnp.pad(packed, ((0, -packed.shape[0] % 8), (0, 0)))


class Sizes:
    def __init__(self, velocity, marker_pos, tiles):
        self.bubbles, _, self.markers = marker_pos.shape
        self.size_x, self.size_y, _, self.tile_len = velocity.shape
        self.touched = tiles.shape[2]
        self.tile_total = self.size_x * self.size_y
        self.width = CAP * self.touched
        assert self.width == self.markers
        self.own_lists = self.bubbles // CAP
        self.n_lists = 26 + self.own_lists
        self.list_row = 6 * self.bubbles + self.n_lists

    def meta(self, blocks):
        rows = -(-(self.n_lists * (CAP + 1)) // self.markers)
        self.meta_len = rows * self.markers
        parts = [b[self.list_row : self.list_row + rows].reshape(-1) for b in blocks]
        return jnp.concatenate(parts).astype(jnp.int32)


def stack_blocks(z, blocks, data, cell):
    cell[...] = lax.broadcasted_iota(jnp.int32, cell.shape, 0).astype(jnp.float32) * scale
    for i, block in enumerate(blocks):
        data[i] = block[...]


def batch_setup(z, tab, meta, meta_at, data, cols, i):
    src, lst = tab[6 * i], tab[6 * i + 1]
    base = (src + meta_at) * z.meta_len
    count = meta[base + z.n_lists * CAP + lst]
    tile_row = data[src, pl.ds(6 * z.bubbles + lst, 1), :]
    tile_x = jnp.floor((tile_row + 0.5) * (1.0 / z.size_y))
    tile_y = tile_row - tile_x * z.size_y
    which = lax.broadcasted_iota(jnp.int32, (8, z.width), 0)
    stacked = jnp.where(
        which == 0, tile_row, jnp.where(which == 1, tile_x * scale, tile_y * scale)
    )
    cols[...] = stacked.T
    shift_x = (tab[6 * i + 3] * z.size_x).astype(jnp.float32)
    shift_y = (tab[6 * i + 4] * z.size_y).astype(jnp.float32)
    shift_z = (tab[6 * i + 5] * z.tile_len).astype(jnp.float32)
    return src, base + lst * CAP, count, tile_row, (shift_x, shift_y, shift_z)


def row_weights(z, data, cols, cell, src, bubble, slot, shifts):
    def coordinate(k):
        return (data[src, pl.ds(k * z.bubbles + bubble, 1), :] - shifts[k]) * scale

    dz = (cell[...] - coordinate(2)).astype(jnp.bfloat16)
    along = jnp.exp2(-(dz * dz))
    mine = cols[pl.ds(slot * z.touched, z.touched), :]
    dx = jnp.broadcast_to(mine[:, 1:2], (z.touched, z.markers)) - coordinate(0)
    dy = jnp.broadcast_to(mine[:, 2:3], (z.touched, z.markers)) - coordinate(1)
    return along, jnp.exp2(-(dx * dx + dy * dy))


def spread_kernel(z, n_blocks, n_init, n_batches, meta_at, *refs):
    tab, meta = refs[:2]
    blocks = refs[2 : 2 + n_blocks]
    inits = refs[2 + n_blocks : 2 + n_blocks + n_init]
    acc, data, cols, cell, pieces = refs[2 + n_blocks + n_init :]
    stack_blocks(z, blocks, data, cell)
    if n_init:
        total = inits[0][...]
        for init in inits[1:]:
            total = total + init[...]
        acc[...] = total
    else:
        acc[...] = jnp.zeros_like(acc)
    pieces[...] = jnp.zeros_like(pieces)

    def batch(i, carry):
        src, first, count, tile_row, shifts = batch_setup(z, tab, meta, meta_at, data, cols, i)
        target = tab[6 * i + 2]

        def rows_of(n):
            for slot in range(n):
                bubble = meta[first + slot]
                along, across = row_weights(z, data, cols, cell, src, bubble, slot, shifts)
                scaled = [
                    (data[src, pl.ds((3 + k) * z.bubbles + bubble, 1), :] * across).astype(
                        jnp.bfloat16
                    )
                    for k in range(3)
                ]
                piece = lax.dot_general(
                    jnp.concatenate(scaled, axis=0),
                    along,
                    (((1,), (1,)), ((), ())),
                    preferred_element_type=jnp.float32,
                ).astype(jnp.bfloat16)
                at = pl.ds(slot * z.touched, z.touched)
                for k in range(3):
                    pieces[at, k * z.tile_len : (k + 1) * z.tile_len] = piece[
                        k * z.touched : (k + 1) * z.touched
                    ]

        least = -1
        for n in STEPS:
            pl.when((count > least) & (count <= n))(functools.partial(rows_of, n))
            least = n
        tile = lax.broadcasted_iota(jnp.int32, (z.tile_total, z.width), 0).astype(jnp.float32)
        placing = (tile == tile_row).astype(jnp.float32).astype(jnp.bfloat16)
        added = jnp.dot(placing, pieces[...], preferred_element_type=jnp.float32)
        for k in range(3):
            acc[target, k] += added[:, k * z.tile_len : (k + 1) * z.tile_len]
        return carry

    lax.fori_loop(0, n_batches, batch, 0)


def cost(z, n_batches):
    rows = n_batches * CAP
    return pl.CostEstimate(
        flops=rows * 2 * 3 * z.touched * z.markers * z.tile_len * 8,
        bytes_accessed=4 << 20,
        transcendentals=rows * z.markers * z.tile_len,
    )


def spread(z, meta, meta_at, blocks, batches, n_acc, inits, name):
    table = jnp.asarray(np.array(batches, np.int32).reshape(-1))
    return pl.pallas_call(
        functools.partial(spread_kernel, z, len(blocks), len(inits), len(batches), meta_at),
        compiler_params=pltpu.CompilerParams(vmem_limit_bytes=VMEM_LIMIT),
        out_shape=jax.ShapeDtypeStruct((n_acc, 3, z.tile_total, z.tile_len), jnp.float32),
        in_specs=[SMEM, SMEM] + [VMEM] * (len(blocks) + len(inits)),
        out_specs=VMEM,
        scratch_shapes=[
            pltpu.VMEM((len(blocks),) + blocks[0].shape, jnp.float32),
            pltpu.VMEM((z.width, 8), jnp.float32),
            pltpu.VMEM((z.tile_len, z.markers), jnp.float32),
            pltpu.VMEM((z.width, 3 * z.tile_len), jnp.bfloat16),
        ],
        cost_estimate=cost(z, len(batches)),
        name=name,
    )(table, meta, *blocks, *inits)


def sample_kernel(z, n_blocks, n_grids, n_init, n_batches, meta_at, *refs):
    tab, meta = refs[:2]
    at = 2 + n_blocks
    blocks = refs[2:at]
    grids = refs[at : at + n_grids]
    inits = refs[at + n_grids : at + n_grids + n_init]
    outs = refs[at + n_grids + n_init : at + n_grids + n_init + n_blocks]
    data, cols, cell, local, low, acc = refs[at + n_grids + n_init + n_blocks :]
    stack_blocks(z, blocks, data, cell)
    for i in range(n_blocks):
        acc[i] = inits[i][...] if n_init else jnp.zeros_like(inits[i] if n_init else outs[i])
    for i, grid in enumerate(grids):
        for k in range(3):
            low[i, :, k * z.tile_len : (k + 1) * z.tile_len] = grid[k].astype(jnp.bfloat16)

    def batch(i, carry):
        src, first, count, _, shifts = batch_setup(z, tab, meta, meta_at, data, cols, i)
        target = tab[6 * i + 2]
        tile = lax.broadcasted_iota(jnp.int32, (z.width, z.tile_total), 1).astype(jnp.float32)
        picking = (jnp.broadcast_to(cols[:, 0:1], tile.shape) == tile).astype(jnp.float32)
        local[...] = jnp.dot(
            picking.astype(jnp.bfloat16), low[target], preferred_element_type=jnp.float32
        ).astype(jnp.bfloat16)

        def rows_of(n):
            for slot in range(n):
                bubble = meta[first + slot]
                along, across = row_weights(z, data, cols, cell, src, bubble, slot, shifts)
                rows = local[pl.ds(slot * z.touched, z.touched), :]
                u = jnp.concatenate(
                    [rows[:, k * z.tile_len : (k + 1) * z.tile_len] for k in range(3)], axis=0
                )
                sampled = jnp.dot(u, along, preferred_element_type=jnp.float32)
                for k in range(3):
                    part = jnp.sum(
                        sampled[k * z.touched : (k + 1) * z.touched] * across,
                        axis=0,
                        keepdims=True,
                    )
                    acc[src, pl.ds(k * z.bubbles + bubble, 1), :] += part

        least = -1
        for n in STEPS:
            pl.when((count > least) & (count <= n))(functools.partial(rows_of, n))
            least = n
        return carry

    lax.fori_loop(0, n_batches, batch, 0)
    for i in range(n_blocks):
        outs[i][...] = acc[i]


def sample(z, meta, meta_at, blocks, grids, batches, inits, name):
    table = jnp.asarray(np.array(batches, np.int32).reshape(-1))
    n = len(blocks)
    shape = (3 * z.bubbles, z.markers)
    return pl.pallas_call(
        functools.partial(sample_kernel, z, n, len(grids), len(inits), len(batches), meta_at),
        compiler_params=pltpu.CompilerParams(vmem_limit_bytes=VMEM_LIMIT),
        out_shape=[jax.ShapeDtypeStruct(shape, jnp.float32)] * n,
        in_specs=[SMEM, SMEM] + [VMEM] * (n + len(grids) + len(inits)),
        out_specs=[VMEM] * n,
        scratch_shapes=[
            pltpu.VMEM((n,) + blocks[0].shape, jnp.float32),
            pltpu.VMEM((z.width, 8), jnp.float32),
            pltpu.VMEM((z.tile_len, z.markers), jnp.float32),
            pltpu.VMEM((z.width, 3 * z.tile_len), jnp.bfloat16),
            pltpu.VMEM((len(grids), z.tile_total, 3 * z.tile_len), jnp.bfloat16),
            pltpu.VMEM((n,) + shape, jnp.float32),
        ],
        cost_estimate=cost(z, len(batches)),
        name=name,
    )(table, meta, *blocks, *grids, *inits)


def smooth_kernel(vel, x_low, x_high, y_low, y_high, out):
    _, size_x, size_y, tile_len = vel.shape
    total = size_x * size_y
    row = lax.broadcasted_iota(jnp.int32, (size_x, size_y, tile_len), 1)
    lane = lax.broadcasted_iota(jnp.int32, (total, tile_len), 1)
    for k in range(3):
        v = vel[k]
        flat = v.reshape(total, tile_len)
        up = jnp.concatenate([x_low[k][None], v[:-1]], axis=0)
        down = jnp.concatenate([v[1:], x_high[k][None]], axis=0)
        left = jnp.where(row == 0, y_low[k][:, None, :], pltpu.roll(v, 1, 1))
        right = jnp.where(row == size_y - 1, y_high[k][:, None, :], pltpu.roll(v, size_y - 1, 1))
        before = pltpu.roll(flat, 1, 1)
        after = pltpu.roll(flat, tile_len - 1, 1)
        near = (up + down + left + right).reshape(total, tile_len)
        near = near + jnp.where(lane == 0, 0.0, before)
        near = near + jnp.where(lane == tile_len - 1, 0.0, after)
        out[0, k] = flat + viscous * (near - 6.0 * flat)
        out[1, k] = jnp.where(lane == tile_len - 1, viscous * after, 0.0)
        out[2, k] = jnp.where(lane == 0, viscous * before, 0.0)


def body(velocity, marker_pos, marker_force, intersect, tiles):
    z = Sizes(velocity, marker_pos, tiles)
    vel = velocity.transpose(2, 0, 1, 3)

    def code(ox, oy, oz):
        return 9 * (ox + 1) + 3 * (oy + 1) + oz + 1

    x_low = shifted(vel[:, -1], "gx", 1)
    x_high = shifted(vel[:, 0], "gx", -1)
    y_low = shifted(vel[:, :, -1], "gy", 1)
    y_high = shifted(vel[:, :, 0], "gy", -1)

    own = message(marker_pos, marker_force, intersect, tiles)
    own, x_low, x_high, y_low, y_high = lax.optimization_barrier(
        (own, x_low, x_high, y_low, y_high)
    )
    if lax.axis_size("gx") == 2:
        x_steps = [(1, (1, -1))]
    else:
        x_steps = [(1, (1,)), (-1, (-1,))]
    x_blocks = [shifted(own, "gx", step) for step, _ in x_steps]
    y_blocks = [shifted(own, "gy", step) for step in (1, -1)]
    xy_blocks = [shifted(block, "gy", step) for step in (1, -1) for block in x_blocks]

    order = {0: 0, -1: 1, 1: 2}

    def own_batches(zs, slot_of):
        found = []
        for oz in zs:
            if oz == 0:
                found += [(0, q, slot_of[0], 0, 0, 0) for q in [13] + list(range(27, z.n_lists))]
            else:
                found.append((0, code(0, 0, oz), slot_of[oz], 0, 0, oz))
        return found

    def x_batches(zs, slot_of, base=0):
        return [
            (base + i, code(ox, 0, oz), slot_of[oz], ox, 0, oz)
            for i, (_, oxs) in enumerate(x_steps)
            for ox in oxs
            for oz in zs
        ]

    def y_batches(zs, slot_of, base=0):
        return [
            (base + i, code(0, oy, oz), slot_of[oz], 0, oy, oz)
            for i, oy in enumerate((1, -1))
            for oz in zs
        ]

    def xy_batches(zs, slot_of, base=0):
        return [
            (base + i * len(x_steps) + j, code(ox, oy, oz), slot_of[oz], ox, oy, oz)
            for i, oy in enumerate((1, -1))
            for j, (_, oxs) in enumerate(x_steps)
            for ox in oxs
            for oz in zs
        ]

    n_x = len(x_steps)
    every, outer, zero, sides = (-1, 1, 0), (-1, 1), {0: 0}, {-1: 0, 1: 1}
    metas = [z.meta([own])]
    acc = spread(z, metas[0], 0, [own], own_batches(every, order), 3, [], "spread_own")
    smooth = pl.pallas_call(
        smooth_kernel,
        out_shape=jax.ShapeDtypeStruct((3, 3, z.tile_total, z.tile_len), jnp.float32),
        in_specs=[VMEM] * 5,
        out_specs=VMEM,
        compiler_params=pltpu.CompilerParams(vmem_limit_bytes=VMEM_LIMIT),
        name="smooth",
    )(vel, x_low, x_high, y_low, y_high)
    mid = x_blocks + y_blocks
    metas.append(z.meta(mid))
    acc = spread(
        z,
        metas[1],
        0,
        mid,
        x_batches(outer, order) + y_batches(outer, order, n_x),
        3,
        [acc, smooth],
        "spread_mid",
    )
    metas.append(z.meta(xy_blocks))
    acc = spread(
        z, metas[2], 0, xy_blocks, xy_batches(outer, order), 3, [acc], "spread_far"
    )
    from_high = shifted(acc[1], "gz", -1)
    from_low = shifted(acc[2], "gz", 1)
    near = [own] + x_blocks
    far = y_blocks + xy_blocks
    meta = jnp.concatenate(metas)
    late = x_batches((0,), zero) + y_batches((0,), zero, n_x) + xy_batches((0,), zero, n_x + 2)
    last = spread(z, meta, 1, x_blocks + far, late, 1, [acc[:1]], "spread_late")
    result = last[0] + from_high + from_low
    low_grid = shifted(result, "gz", 1)
    high_grid = shifted(result, "gz", -1)
    velocity_out = result.reshape(3, z.size_x, z.size_y, z.tile_len).transpose(1, 2, 0, 3)

    here = (
        own_batches((0,), zero)
        + x_batches((0,), zero, 1)
        + y_batches((0,), zero, 1 + n_x)
        + xy_batches((0,), zero, 3 + n_x)
    )
    part = sample(z, meta, 0, near + far, [result], here, [], "sample_here")
    far_part = sample(
        z,
        meta,
        1 + n_x,
        far,
        [low_grid, high_grid],
        y_batches(outer, sides) + xy_batches(outer, sides, 2),
        part[1 + n_x :],
        "sample_far",
    )
    xy_back = [
        shifted(far_part[2 + i * n_x + j], "gy", -oy) for i, oy in enumerate((1, -1)) for j in range(n_x)
    ]
    y_back = [shifted(far_part[i], "gy", -oy) for i, oy in enumerate((1, -1))]
    near_part = sample(
        z,
        meta,
        0,
        near,
        [low_grid, high_grid],
        own_batches(outer, sides) + x_batches(outer, sides, 1),
        part[: 1 + n_x],
        "sample_near",
    )
    total = near_part[0]
    for j, (step, _) in enumerate(x_steps):
        side = near_part[1 + j] + xy_back[j] + xy_back[n_x + j]
        total = total + shifted(side, "gx", -step)
    total = total + y_back[0] + y_back[1]
    marker_velocity = total.reshape(3, z.bubbles, z.markers).transpose(1, 0, 2)
    return (velocity_out, marker_velocity)


def solution(mesh):
    rows = P(("gx", "gy", "gz"), None, None)
    grid = P("gx", "gy", None, "gz")
    return jax.shard_map(
        body,
        mesh=mesh,
        in_specs=(grid, rows, rows, P(("gx", "gy", "gz"), None), rows),
        out_specs=(grid, rows),
        check_vma=False,
    )
```

profile of v0, /device:TPU:0, one launch (start us, length us, event | category | flops | bytes accessed | tf_op | source)
XLA Modules:
  0.0 109.3 jit_solution(11792280814654403862)
XLA Ops:
  0.7 1.2 %copy.44 = f32[16,16,3,128]{3,0,2,1:T(8,128)S(1)} copy(f32[16,16,3,128]{3,1,2,0:T(8,128)} %param.12) | data formatting | bytes 786432 | tf_op args[0]
  1.9 3.1 %collective-permute-start = (f32[3,16,128]{2,1,0:T(8,128)S(1)}, f32[3,16,128]{2,1,0:T(8,128)S(1)}, u32[]{:S(2)}, u32[]{:S(2)}) collective-permute-start(f32[3,16,128]{2,1,0:T(8,128)S(1)} %bitcast.73), channel_id=1, source_target_pairs={{0,16},{16,0},{1,17},{17,1},{2,18},{18,2},{3,19},{19,3},{4,20},{20... | collective-permute-start | bytes 73736 | tf_op jit(solution)/shard_map/ppermute | solution.py:25
  5.0 1.7 %collective-permute-start.3 = (f32[3,16,128]{2,1,0:T(8,128)S(1)}, f32[3,16,128]{2,1,0:T(8,128)S(1)}, u32[]{:S(2)}, u32[]{:S(2)}) collective-permute-start(f32[3,16,128]{2,1,0:T(8,128)S(1)} %get-tuple-element.39), channel_id=1, source_target_pairs={{0,12},{4,0},{8,4},{12,8},{1,13},{5,1},{9,5},{13,9},{2,14},{6,2},{... | collective-permute-start | bytes 73736 | tf_op jit(solution)/shard_map/ppermute | solution.py:25
  10.7 2.0 %collective-permute-start.4 = (f32[416,256]{1,0:T(8,128)S(1)}, f32[416,256]{1,0:T(8,128)S(1)}, u32[]{:S(2)}, u32[]{:S(2)}) collective-permute-start(f32[416,256]{1,0:T(8,128)S(1)} %concatenate.20.refs_2_), channel_id=1, source_target_pairs={{0,16},{16,0},{1,17},{17,1},{2,18},{18,2},{3,19},{19,3},{4,20},{20... | collective-permute-start | bytes 1277960 | tf_op jit(solution)/shard_map/ppermute | solution.py:25
  12.8 1.7 %collective-permute-start.6 = (f32[416,256]{1,0:T(8,128)S(1)}, f32[416,256]{1,0:T(8,128)S(1)}, u32[]{:S(2)}, u32[]{:S(2)}) collective-permute-start(f32[416,256]{1,0:T(8,128)S(1)} %concatenate.20.refs_2_), channel_id=1, source_target_pairs={{0,12},{4,0},{8,4},{12,8},{1,13},{5,1},{9,5},{13,9},{2,14},{6,2},{... | collective-permute-start | bytes 1277960 | tf_op jit(solution)/shard_map/ppermute | solution.py:25
  14.8 5.7 %spread_own.1.refs_5_ = f32[3,3,256,128]{3,2,1,0:T(8,128)S(1)} custom-call(s32[36]{0:T(128)S(1)} %copy-done.6, s32[512]{0:T(512)S(1)} %bitcast.63, f32[416,256]{1,0:T(8,128)S(1)} %concatenate.20.refs_2_), custom_call_target="tpu_custom_call" | custom-call | flops 2415919104 | bytes 4194304 | tf_op jit(solution)/shard_map/spread_own/pallas_call | solution.py:188
  20.6 2.2 %collective-permute-done.4.refs_2_.refs_3_ = f32[416,256]{1,0:T(8,128)S(1)} collective-permute-done((f32[416,256]{1,0:T(8,128)S(1)}, f32[416,256]{1,0:T(8,128)S(1)}, u32[]{:S(2)}, u32[]{:S(2)}) %collective-permute-start.4) | collective-permute-done | bytes 426016 | tf_op jit(solution)/shard_map/ppermute | solution.py:25
  24.0 2.3 %collective-permute-start.8 = (f32[416,256]{1,0:T(8,128)S(1)}, f32[416,256]{1,0:T(8,128)S(1)}, u32[]{:S(2)}, u32[]{:S(2)}) collective-permute-start(f32[416,256]{1,0:T(8,128)S(1)} %collective-permute-done.4.refs_2_.refs_3_), channel_id=1, source_target_pairs={{0,12},{4,0},{8,4},{12,8},{1,13},{5,1},{9,5},{13,9},{2,14},{6,2},{... | collective-permute-start | bytes 1277960 | tf_op jit(solution)/shard_map/ppermute | solution.py:25
  26.3 6.4 %spread_mid.1.refs_4_ = f32[3,3,256,128]{3,2,1,0:T(8,128)S(1)} custom-call(s32[48]{0:T(128)S(1)} %copy-done.5, s32[1536]{0:T(1024)S(1)} %maximum_convert_fusion.refs_1_, f32[416,256]{1,0:T(8,128)S(1)} %collective-permute-done.4.refs_2_.refs_3_, f32[416,256]{1,0:T(8,128)S(1)} %collective-permute-done.5.refs_3_.refs_4_.refs_2_, ...), custom_call_target="tpu_custom_call" | custom-call | flops 3221225472 | bytes 4194304 | tf_op jit(solution)/shard_map/spread_mid/pallas_call | solution.py:188
  33.0 6.1 %spread_far.1 = f32[3,3,256,128]{3,2,1,0:T(8,128)S(1)} custom-call(s32[48]{0:T(128)S(1)} %copy-done.4, s32[1024]{0:T(1024)S(1)} %maximum_convert_fusion.1.refs_1_, f32[416,256]{1,0:T(8,128)S(1)} %collective-permute-done.7.refs_2_.refs_5_.refs_6_.refs_4_, f32[416,256]{1,0:T(8,128)S(1)} %collective-permute-done.8.refs_3_.refs_6_.refs_7_.refs_5_, ...), custom_call_target="tpu_custom_call" | custom-call | flops 3221225472 | bytes 4194304 | tf_op jit(solution)/shard_map/spread_far/pallas_call | solution.py:188
  39.3 5.4 %collective-permute-start.10 = (f32[3,256,128]{2,1,0:T(8,128)S(1)}, f32[3,256,128]{2,1,0:T(8,128)S(1)}, u32[]{:S(2)}, u32[]{:S(2)}) collective-permute-start(f32[3,256,128]{2,1,0:T(8,128)S(1)} %get-tuple-element.37), channel_id=1, source_target_pairs={{0,1},{1,2},{2,3},{3,0},{4,5},{5,6},{6,7},{7,4},{8,9},{9,10},{10,1... | collective-permute-start | bytes 1179656 | tf_op jit(solution)/shard_map/ppermute | solution.py:25
  44.7 2.1 %collective-permute-start.9 = (f32[3,256,128]{2,1,0:T(8,128)S(1)}, f32[3,256,128]{2,1,0:T(8,128)S(1)}, u32[]{:S(2)}, u32[]{:S(2)}) collective-permute-start(f32[3,256,128]{2,1,0:T(8,128)S(1)} %get-tuple-element.38), channel_id=1, source_target_pairs={{0,3},{1,0},{2,1},{3,2},{4,7},{5,4},{6,5},{7,6},{8,11},{9,8},{10,9... | collective-permute-start | bytes 1179656 | tf_op jit(solution)/shard_map/ppermute | solution.py:25
  46.8 8.5 %spread_late.1 = f32[1,3,256,128]{3,2,1,0:T(8,128)S(1)} custom-call(s32[48]{0:T(128)S(1)} %copy-done.3, s32[3072]{0:T(1024)S(1)} %pad_add_fusion.1.refs_1_, f32[416,256]{1,0:T(8,128)S(1)} %collective-permute-done.4.refs_2_.refs_3_, f32[416,256]{1,0:T(8,128)S(1)} %collective-permute-done.5.refs_3_.refs_4_.refs_2_, ...), custom_call_target="tpu_custom_call" | custom-call | flops 3221225472 | bytes 4194304 | tf_op jit(solution)/shard_map/spread_late/pallas_call | solution.py:188
  55.3 1.4 %collective-permute-done.10 = f32[3,256,128]{2,1,0:T(8,128)S(1)} collective-permute-done((f32[3,256,128]{2,1,0:T(8,128)S(1)}, f32[3,256,128]{2,1,0:T(8,128)S(1)}, u32[]{:S(2)}, u32[]{:S(2)}) %collective-permute-start.10) | collective-permute-done | bytes 393248 | tf_op jit(solution)/shard_map/ppermute | solution.py:25
  56.8 6.2 %collective-permute-done.9 = f32[3,256,128]{2,1,0:T(8,128)S(1)} collective-permute-done((f32[3,256,128]{2,1,0:T(8,128)S(1)}, f32[3,256,128]{2,1,0:T(8,128)S(1)}, u32[]{:S(2)}, u32[]{:S(2)}) %collective-permute-start.9) | collective-permute-done | bytes 393248 | tf_op jit(solution)/shard_map/ppermute | solution.py:25
  63.1 1.2 %collective-permute-start.11 = (f32[3,256,128]{2,1,0:T(8,128)S(1)}, f32[3,256,128]{2,1,0:T(8,128)S(1)}, u32[]{:S(2)}, u32[]{:S(2)}) collective-permute-start(f32[3,256,128]{2,1,0:T(8,128)S(1)} %fusion.refs_8_), channel_id=1, source_target_pairs={{0,1},{1,2},{2,3},{3,0},{4,5},{5,6},{6,7},{7,4},{8,9},{9,10},{10,1... | collective-permute-start | bytes 1179656 | tf_op jit(solution)/shard_map/ppermute | solution.py:25
  64.3 2.7 %collective-permute-start.12 = (f32[3,256,128]{2,1,0:T(8,128)S(1)}, f32[3,256,128]{2,1,0:T(8,128)S(1)}, u32[]{:S(2)}, u32[]{:S(2)}) collective-permute-start(f32[3,256,128]{2,1,0:T(8,128)S(1)} %fusion.refs_8_), channel_id=1, source_target_pairs={{0,3},{1,0},{2,1},{3,2},{4,7},{5,4},{6,5},{7,6},{8,11},{9,8},{10,9... | collective-permute-start | bytes 1179656 | tf_op jit(solution)/shard_map/ppermute | solution.py:25
  66.9 13.6 %sample_here.1 = (f32[192,256]{1,0:T(8,128)S(1)}, f32[192,256]{1,0:T(8,128)S(1)}, f32[192,256]{1,0:T(8,128)S(1)}, f32[192,256]{1,0:T(8,128)S(1)}, f32[192,256]{1,0:T(8,128)S(1)}, /*index=5*/f32[192,256]{1,0:T(8,128)S(1)}) custom-call(s32[72]{0:T(128)S(1)} %copy-done.2, s32[3072]{0:T(1024)S(1)} %pad_add_fusion.1.refs_1_, f32[416,256]{1,0:T(8,128)S(1)} %concatenate.20.refs_2_, ...), custom_call_target="tpu_custom_call" | custom-call | flops 4831838208 | bytes 4194304 | tf_op jit(solution)/shard_map/sample_here/pallas_call | solution.py:261
  80.6 2.9 %collective-permute-done.12.refs_5_.refs_7_ = f32[3,256,128]{2,1,0:T(8,128)S(1)} collective-permute-done((f32[3,256,128]{2,1,0:T(8,128)S(1)}, f32[3,256,128]{2,1,0:T(8,128)S(1)}, u32[]{:S(2)}, u32[]{:S(2)}) %collective-permute-start.12) | collective-permute-done | bytes 393248 | tf_op jit(solution)/shard_map/ppermute | solution.py:25
  83.5 9.8 %sample_far.1 = (f32[192,256]{1,0:T(8,128)S(1)}, f32[192,256]{1,0:T(8,128)S(1)}, f32[192,256]{1,0:T(8,128)S(1)}, f32[192,256]{1,0:T(8,128)S(1)}) custom-call(s32[72]{0:T(128)S(1)} %copy-done.1, s32[3072]{0:T(1024)S(1)} %pad_add_fusion.1.refs_1_, f32[416,256]{1,0:T(8,128)S(1)} %collective-permute-done.5.refs_3_.refs_4_.refs_2_, ...), custom_call_target="tpu_custom_call" | custom-call | flops 4831838208 | bytes 4194304 | tf_op jit(solution)/shard_map/sample_far/pallas_call | solution.py:261
  93.3 1.8 %collective-permute-start.14 = (f32[192,256]{1,0:T(8,128)S(1)}, f32[192,256]{1,0:T(8,128)S(1)}, u32[]{:S(2)}, u32[]{:S(2)}) collective-permute-start(f32[192,256]{1,0:T(8,128)S(1)} %get-tuple-element.33), channel_id=1, source_target_pairs={{0,4},{4,8},{8,12},{12,0},{1,5},{5,9},{9,13},{13,1},{2,6},{6,10},{... | collective-permute-start | bytes 589832 | tf_op jit(solution)/shard_map/ppermute | solution.py:25
  95.1 1.7 %collective-permute-start.17 = (f32[192,256]{1,0:T(8,128)S(1)}, f32[192,256]{1,0:T(8,128)S(1)}, u32[]{:S(2)}, u32[]{:S(2)}) collective-permute-start(f32[192,256]{1,0:T(8,128)S(1)} %get-tuple-element.35), channel_id=1, source_target_pairs={{0,4},{4,8},{8,12},{12,0},{1,5},{5,9},{9,13},{13,1},{2,6},{6,10},{... | collective-permute-start | bytes 589832 | tf_op jit(solution)/shard_map/ppermute | solution.py:25
  96.8 5.3 %sample_near.1 = (f32[192,256]{1,0:T(8,128)S(1)}, f32[192,256]{1,0:T(8,128)S(1)}) custom-call(s32[36]{0:T(128)S(1)} %copy-done, s32[3072]{0:T(1024)S(1)} %pad_add_fusion.1.refs_1_, f32[416,256]{1,0:T(8,128)S(1)} %concatenate.20.refs_2_, f32[416,256]{1,0:T(8,128)S(1)} %collective-permute-done.4.refs_2_.refs_3_, ...), custom_call_target="tpu_custom_call" | custom-call | flops 2415919104 | bytes 4194304 | tf_op jit(solution)/shard_map/sample_near/pallas_call | solution.py:261
  103.1 5.4 %collective-permute-done.15 = f32[192,256]{1,0:T(8,128)S(1)} collective-permute-done((f32[192,256]{1,0:T(8,128)S(1)}, f32[192,256]{1,0:T(8,128)S(1)}, u32[]{:S(2)}, u32[]{:S(2)}) %collective-permute-start.15) | collective-permute-done | bytes 196640 | tf_op jit(solution)/shard_map/ppermute | solution.py:25
  (102 shorter events, 7.6 us)
Async XLA Ops:
  0.6 8.7 %copy-start.8 = (s32[64,27,16]{0,2,1:T(8,128)S(1)}, s32[64,27,16]{0,2,1:T(8,128)}, u32[]{:S(2)}) copy-start(s32[64,27,16]{0,2,1:T(8,128)} %param.16) | copy-start | bytes 331780
  1.8 8.6 %copy-start.7 = (f32[16,16,3,128]{3,1,2,0:T(8,128)S(1)}, f32[16,16,3,128]{3,1,2,0:T(8,128)}, u32[]{:S(2)}) copy-start(f32[16,16,3,128]{3,1,2,0:T(8,128)} %param.12) | copy-start | bytes 1179652
  1.9 8.8 %collective-permute-start = (f32[3,16,128]{2,1,0:T(8,128)S(1)}, f32[3,16,128]{2,1,0:T(8,128)S(1)}, u32[]{:S(2)}, u32[]{:S(2)}) collective-permute-start(f32[3,16,128]{2,1,0:T(8,128)S(1)} %bitcast.73), channel_id=1, source_target_pairs={{0,16},{16,0},{1,17},{17,1},{2,18},{18,2},{3,19},{19,3},{4,20},{20... | collective-permute-start | bytes 73736 | tf_op jit(solution)/shard_map/ppermute | solution.py:25
  5.0 5.8 %collective-permute-start.1 = (f32[3,16,128]{2,1,0:T(8,128)S(1)}, f32[3,16,128]{2,1,0:T(8,128)S(1)}, u32[]{:S(2)}, u32[]{:S(2)}) collective-permute-start(f32[3,16,128]{2,1,0:T(8,128)S(1)} %bitcast.74), channel_id=1, source_target_pairs={{0,16},{16,0},{1,17},{17,1},{2,18},{18,2},{3,19},{19,3},{4,20},{20... | collective-permute-start | bytes 73736 | tf_op jit(solution)/shard_map/ppermute | solution.py:25
  5.0 5.7 %collective-permute-start.2 = (f32[3,16,128]{2,1,0:T(8,128)S(1)}, f32[3,16,128]{2,1,0:T(8,128)S(1)}, u32[]{:S(2)}, u32[]{:S(2)}) collective-permute-start(f32[3,16,128]{2,1,0:T(8,128)S(1)} %get-tuple-element.40), channel_id=1, source_target_pairs={{0,4},{4,8},{8,12},{12,0},{1,5},{5,9},{9,13},{13,1},{2,6},{6,10},{... | collective-permute-start | bytes 73736 | tf_op jit(solution)/shard_map/ppermute | solution.py:25
  5.0 5.7 %collective-permute-start.3 = (f32[3,16,128]{2,1,0:T(8,128)S(1)}, f32[3,16,128]{2,1,0:T(8,128)S(1)}, u32[]{:S(2)}, u32[]{:S(2)}) collective-permute-start(f32[3,16,128]{2,1,0:T(8,128)S(1)} %get-tuple-element.39), channel_id=1, source_target_pairs={{0,12},{4,0},{8,4},{12,8},{1,13},{5,1},{9,5},{13,9},{2,14},{6,2},{... | collective-permute-start | bytes 73736 | tf_op jit(solution)/shard_map/ppermute | solution.py:25
  10.7 12.1 %collective-permute-start.4 = (f32[416,256]{1,0:T(8,128)S(1)}, f32[416,256]{1,0:T(8,128)S(1)}, u32[]{:S(2)}, u32[]{:S(2)}) collective-permute-start(f32[416,256]{1,0:T(8,128)S(1)} %concatenate.20.refs_2_), channel_id=1, source_target_pairs={{0,16},{16,0},{1,17},{17,1},{2,18},{18,2},{3,19},{19,3},{4,20},{20... | collective-permute-start | bytes 1277960 | tf_op jit(solution)/shard_map/ppermute | solution.py:25
  12.7 10.3 %collective-permute-start.5 = (f32[416,256]{1,0:T(8,128)S(1)}, f32[416,256]{1,0:T(8,128)S(1)}, u32[]{:S(2)}, u32[]{:S(2)}) collective-permute-start(f32[416,256]{1,0:T(8,128)S(1)} %concatenate.20.refs_2_), channel_id=1, source_target_pairs={{0,4},{4,8},{8,12},{12,0},{1,5},{5,9},{9,13},{13,1},{2,6},{6,10},{... | collective-permute-start | bytes 1277960 | tf_op jit(solution)/shard_map/ppermute | solution.py:25
  12.8 11.2 %collective-permute-start.6 = (f32[416,256]{1,0:T(8,128)S(1)}, f32[416,256]{1,0:T(8,128)S(1)}, u32[]{:S(2)}, u32[]{:S(2)}) collective-permute-start(f32[416,256]{1,0:T(8,128)S(1)} %concatenate.20.refs_2_), channel_id=1, source_target_pairs={{0,12},{4,0},{8,4},{12,8},{1,13},{5,1},{9,5},{13,9},{2,14},{6,2},{... | collective-permute-start | bytes 1277960 | tf_op jit(solution)/shard_map/ppermute | solution.py:25
  14.8 11.4 %copy-start.5 = (s32[48]{0:T(128)S(1)}, s32[48]{0:T(128)}, u32[]{:S(2)}) copy-start(s32[48]{0:T(128)} %constant.35.clone.refs_0_) | copy-start | bytes 580
  22.8 10.0 %collective-permute-start.7 = (f32[416,256]{1,0:T(8,128)S(1)}, f32[416,256]{1,0:T(8,128)S(1)}, u32[]{:S(2)}, u32[]{:S(2)}) collective-permute-start(f32[416,256]{1,0:T(8,128)S(1)} %collective-permute-done.4.refs_2_.refs_3_), channel_id=1, source_target_pairs={{0,4},{4,8},{8,12},{12,0},{1,5},{5,9},{9,13},{13,1},{2,6},{6,10},{... | collective-permute-start | bytes 1277960 | tf_op jit(solution)/shard_map/ppermute | solution.py:25
  24.0 9.0 %collective-permute-start.8 = (f32[416,256]{1,0:T(8,128)S(1)}, f32[416,256]{1,0:T(8,128)S(1)}, u32[]{:S(2)}, u32[]{:S(2)}) collective-permute-start(f32[416,256]{1,0:T(8,128)S(1)} %collective-permute-done.4.refs_2_.refs_3_), channel_id=1, source_target_pairs={{0,12},{4,0},{8,4},{12,8},{1,13},{5,1},{9,5},{13,9},{2,14},{6,2},{... | collective-permute-start | bytes 1277960 | tf_op jit(solution)/shard_map/ppermute | solution.py:25
  39.3 17.5 %collective-permute-start.10 = (f32[3,256,128]{2,1,0:T(8,128)S(1)}, f32[3,256,128]{2,1,0:T(8,128)S(1)}, u32[]{:S(2)}, u32[]{:S(2)}) collective-permute-start(f32[3,256,128]{2,1,0:T(8,128)S(1)} %get-tuple-element.37), channel_id=1, source_target_pairs={{0,1},{1,2},{2,3},{3,0},{4,5},{5,6},{6,7},{7,4},{8,9},{9,10},{10,1... | collective-permute-start | bytes 1179656 | tf_op jit(solution)/shard_map/ppermute | solution.py:25
  44.7 18.2 %collective-permute-start.9 = (f32[3,256,128]{2,1,0:T(8,128)S(1)}, f32[3,256,128]{2,1,0:T(8,128)S(1)}, u32[]{:S(2)}, u32[]{:S(2)}) collective-permute-start(f32[3,256,128]{2,1,0:T(8,128)S(1)} %get-tuple-element.38), channel_id=1, source_target_pairs={{0,3},{1,0},{2,1},{3,2},{4,7},{5,4},{6,5},{7,6},{8,11},{9,8},{10,9... | collective-permute-start | bytes 1179656 | tf_op jit(solution)/shard_map/ppermute | solution.py:25
  55.3 11.6 %copy-start.2 = (s32[72]{0:T(128)S(1)}, s32[72]{0:T(128)}, u32[]{:S(2)}) copy-start(s32[72]{0:T(128)} %constant.38.clone.refs_0_) | copy-start | bytes 868
  63.0 20.4 %copy-start.1 = (s32[72]{0:T(128)S(1)}, s32[72]{0:T(128)}, u32[]{:S(2)}) copy-start(s32[72]{0:T(128)} %constant.39.clone.refs_0_) | copy-start | bytes 868
  63.1 17.5 %collective-permute-start.11 = (f32[3,256,128]{2,1,0:T(8,128)S(1)}, f32[3,256,128]{2,1,0:T(8,128)S(1)}, u32[]{:S(2)}, u32[]{:S(2)}) collective-permute-start(f32[3,256,128]{2,1,0:T(8,128)S(1)} %fusion.refs_8_), channel_id=1, source_target_pairs={{0,1},{1,2},{2,3},{3,0},{4,5},{5,6},{6,7},{7,4},{8,9},{9,10},{10,1... | collective-permute-start | bytes 1179656 | tf_op jit(solution)/shard_map/ppermute | solution.py:25
  64.3 19.2 %collective-permute-start.12 = (f32[3,256,128]{2,1,0:T(8,128)S(1)}, f32[3,256,128]{2,1,0:T(8,128)S(1)}, u32[]{:S(2)}, u32[]{:S(2)}) collective-permute-start(f32[3,256,128]{2,1,0:T(8,128)S(1)} %fusion.refs_8_), channel_id=1, source_target_pairs={{0,3},{1,0},{2,1},{3,2},{4,7},{5,4},{6,5},{7,6},{8,11},{9,8},{10,9... | collective-permute-start | bytes 1179656 | tf_op jit(solution)/shard_map/ppermute | solution.py:25
  83.5 13.4 %copy-start = (s32[36]{0:T(128)S(1)}, s32[36]{0:T(128)}, u32[]{:S(2)}) copy-start(s32[36]{0:T(128)} %constant.40.clone.refs_0_) | copy-start | bytes 436
  93.3 8.9 %collective-permute-start.13 = (f32[192,256]{1,0:T(8,128)S(1)}, f32[192,256]{1,0:T(8,128)S(1)}, u32[]{:S(2)}, u32[]{:S(2)}) collective-permute-start(f32[192,256]{1,0:T(8,128)S(1)} %get-tuple-element.32), channel_id=1, source_target_pairs={{0,12},{4,0},{8,4},{12,8},{1,13},{5,1},{9,5},{13,9},{2,14},{6,2},{... | collective-permute-start | bytes 589832 | tf_op jit(solution)/shard_map/ppermute | solution.py:25
  93.3 8.9 %collective-permute-start.14 = (f32[192,256]{1,0:T(8,128)S(1)}, f32[192,256]{1,0:T(8,128)S(1)}, u32[]{:S(2)}, u32[]{:S(2)}) collective-permute-start(f32[192,256]{1,0:T(8,128)S(1)} %get-tuple-element.33), channel_id=1, source_target_pairs={{0,4},{4,8},{8,12},{12,0},{1,5},{5,9},{9,13},{13,1},{2,6},{6,10},{... | collective-permute-start | bytes 589832 | tf_op jit(solution)/shard_map/ppermute | solution.py:25
  95.1 8.0 %collective-permute-start.16 = (f32[192,256]{1,0:T(8,128)S(1)}, f32[192,256]{1,0:T(8,128)S(1)}, u32[]{:S(2)}, u32[]{:S(2)}) collective-permute-start(f32[192,256]{1,0:T(8,128)S(1)} %get-tuple-element.34), channel_id=1, source_target_pairs={{0,12},{4,0},{8,4},{12,8},{1,13},{5,1},{9,5},{13,9},{2,14},{6,2},{... | collective-permute-start | bytes 589832 | tf_op jit(solution)/shard_map/ppermute | solution.py:25
  95.1 8.0 %collective-permute-start.17 = (f32[192,256]{1,0:T(8,128)S(1)}, f32[192,256]{1,0:T(8,128)S(1)}, u32[]{:S(2)}, u32[]{:S(2)}) collective-permute-start(f32[192,256]{1,0:T(8,128)S(1)} %get-tuple-element.35), channel_id=1, source_target_pairs={{0,4},{4,8},{8,12},{12,0},{1,5},{5,9},{9,13},{13,1},{2,6},{6,10},{... | collective-permute-start | bytes 589832 | tf_op jit(solution)/shard_map/ppermute | solution.py:25
  102.3 6.3 %collective-permute-start.15 = (f32[192,256]{1,0:T(8,128)S(1)}, f32[192,256]{1,0:T(8,128)S(1)}, u32[]{:S(2)}, u32[]{:S(2)}) collective-permute-start(f32[192,256]{1,0:T(8,128)S(1)} %add_add_fusion.1), channel_id=1, source_target_pairs={{0,16},{16,0},{1,17},{17,1},{2,18},{18,2},{3,19},{19,3},{4,20},{20... | collective-permute-start | bytes 589832 | tf_op jit(solution)/shard_map/ppermute | solution.py:25
  (6 other events, 30.2 us)
where the time goes:
time: 111 us; the launch traced here: 109 us
  Pallas kernels  55.9 us (50%)
  starting transfers between devices  25.9 us (23%)
  waiting for transfers between devices  19.6 us (18%)
  local copies, waits for them, and re-layouts  4.17 us (4%)
  other arithmetic  2.49 us (2%)
    pallas_call x3, Pallas kernels, sample(): pl.pallas_call(functools.partial(sample_kernel, z, n, len(grids), len(ini...  28.8 us
    pallas_call x4, Pallas kernels, spread(): pl.pallas_call(functools.partial(spread_kernel, z, len(blocks), len(inits...  26.8 us
    ppermute x18, starting transfers between devices, shifted(): lax.ppermute(value, axis, [(i, (i + step) % count) for i in range(count)])  25.9 us
    ppermute x18, waiting for transfers between devices, shifted(): lax.ppermute(value, axis, [(i, (i + step) % count) for i in range(count)])  19.6 us
  transfers between devices with their start and end apart: 18, of which 9 were waited for; matrix products, arithmetic and copies ran while one was open for 4% of the time, Pallas kernels for 37%

commit v1 on v0

--- a/solution.py
+++ b/solution.py
@@ -419,19 +419,29 @@
         shifted(far_part[2 + i * n_x + j], "gy", -oy) for i, oy in enumerate((1, -1)) for j in range(n_x)
     ]
     y_back = [shifted(far_part[i], "gy", -oy) for i, oy in enumerate((1, -1))]
-    near_part = sample(
+    side_part = sample(
+        z,
+        meta,
+        1,
+        x_blocks,
+        [low_grid, high_grid],
+        x_batches(outer, sides),
+        part[1 : 1 + n_x],
+        "sample_side",
+    )
+    own_part = sample(
         z,
         meta,
         0,
-        near,
+        [own],
         [low_grid, high_grid],
-        own_batches(outer, sides) + x_batches(outer, sides, 1),
-        part[: 1 + n_x],
-        "sample_near",
-    )
-    total = near_part[0]
+        own_batches(outer, sides),
+        part[:1],
+        "sample_own",
+    )
+    total = own_part[0]
     for j, (step, _) in enumerate(x_steps):
-        side = near_part[1 + j] + xy_back[j] + xy_back[n_x + j]
+        side = side_part[j] + xy_back[j] + xy_back[n_x + j]
         total = total + shifted(side, "gx", -step)
     total = total + y_back[0] + y_back[1]
     marker_velocity = total.reshape(3, z.bubbles, z.markers).transpose(1, 0, 2)

time: 111 us -> 110 us (level)
  Pallas kernels: 55.9 us -> 51.8 us
  waiting for transfers between devices: 19.6 us -> 21.3 us
    pallas_call x4, Pallas kernels: 26.8 us -> 24.6 us  [spread(): pl.pallas_call(functools.partial(spread_kernel, z, len(blocks), len(inits...]
    pallas_call x3 -> x4, Pallas kernels: 28.8 us -> 27 us  [sample(): pl.pallas_call(functools.partial(sample_kernel, z, n, len(grids), len(ini...]
    ppermute x18, waiting for transfers between devices: 19.6 us -> 21.3 us  [shifted(): lax.ppermute(value, axis, [(i, (i + step) % count) for i in range(count)])]
  transfers between devices with their start and end apart: 18 -> 18, of which waited for: 9 -> 10; matrix products, arithmetic and copies ran while one was open for 4% -> 4% of each run, Pallas kernels for 37% -> 34%
where the time goes in v1:
time: 110 us; the launch traced here: 108 us
  Pallas kernels  51.8 us (47%)
  starting transfers between devices  26.8 us (24%)
  waiting for transfers between devices  21.3 us (19%)
  local copies, waits for them, and re-layouts  4.17 us (4%)
  other arithmetic  2.49 us (2%)
    pallas_call x4, Pallas kernels, sample(): pl.pallas_call(functools.partial(sample_kernel, z, n, len(grids), len(ini...  27 us
    ppermute x18, starting transfers between devices, shifted(): lax.ppermute(value, axis, [(i, (i + step) % count) for i in range(count)])  26.8 us
    pallas_call x4, Pallas kernels, spread(): pl.pallas_call(functools.partial(spread_kernel, z, len(blocks), len(inits...  24.6 us
    ppermute x18, waiting for transfers between devices, shifted(): lax.ppermute(value, axis, [(i, (i + step) % count) for i in range(count)])  21.3 us
  transfers between devices with their start and end apart: 18, of which 10 were waited for; matrix products, arithmetic and copies ran while one was open for 4% of the time, Pallas kernels for 34%

profile of v1, /device:TPU:0, one launch (start us, length us, event | category | flops | bytes accessed | tf_op | source)
XLA Modules:
  0.0 107.8 jit_solution(4854727852094091420)
XLA Ops:
  0.7 1.2 %copy.45 = f32[16,16,3,128]{3,0,2,1:T(8,128)S(1)} copy(f32[16,16,3,128]{3,1,2,0:T(8,128)} %param.13) | data formatting | bytes 786432 | tf_op args[0]
  1.9 3.1 %collective-permute-start = (f32[3,16,128]{2,1,0:T(8,128)S(1)}, f32[3,16,128]{2,1,0:T(8,128)S(1)}, u32[]{:S(2)}, u32[]{:S(2)}) collective-permute-start(f32[3,16,128]{2,1,0:T(8,128)S(1)} %bitcast.73), channel_id=1, source_target_pairs={{0,16},{16,0},{1,17},{17,1},{2,18},{18,2},{3,19},{19,3},{4,20},{20... | collective-permute-start | bytes 73736 | tf_op jit(solution)/shard_map/ppermute | solution.py:25
  5.0 1.7 %collective-permute-start.3 = (f32[3,16,128]{2,1,0:T(8,128)S(1)}, f32[3,16,128]{2,1,0:T(8,128)S(1)}, u32[]{:S(2)}, u32[]{:S(2)}) collective-permute-start(f32[3,16,128]{2,1,0:T(8,128)S(1)} %get-tuple-element.35), channel_id=1, source_target_pairs={{0,12},{4,0},{8,4},{12,8},{1,13},{5,1},{9,5},{13,9},{2,14},{6,2},{... | collective-permute-start | bytes 73736 | tf_op jit(solution)/shard_map/ppermute | solution.py:25
  10.7 2.0 %collective-permute-start.4 = (f32[416,256]{1,0:T(8,128)S(1)}, f32[416,256]{1,0:T(8,128)S(1)}, u32[]{:S(2)}, u32[]{:S(2)}) collective-permute-start(f32[416,256]{1,0:T(8,128)S(1)} %concatenate.20.refs_2_), channel_id=1, source_target_pairs={{0,16},{16,0},{1,17},{17,1},{2,18},{18,2},{3,19},{19,3},{4,20},{20... | collective-permute-start | bytes 1277960 | tf_op jit(solution)/shard_map/ppermute | solution.py:25
  12.8 1.7 %collective-permute-start.6 = (f32[416,256]{1,0:T(8,128)S(1)}, f32[416,256]{1,0:T(8,128)S(1)}, u32[]{:S(2)}, u32[]{:S(2)}) collective-permute-start(f32[416,256]{1,0:T(8,128)S(1)} %concatenate.20.refs_2_), channel_id=1, source_target_pairs={{0,12},{4,0},{8,4},{12,8},{1,13},{5,1},{9,5},{13,9},{2,14},{6,2},{... | collective-permute-start | bytes 1277960 | tf_op jit(solution)/shard_map/ppermute | solution.py:25
  14.8 5.8 %spread_own.1.refs_5_ = f32[3,3,256,128]{3,2,1,0:T(8,128)S(1)} custom-call(s32[36]{0:T(128)S(1)} %copy-done.7, s32[512]{0:T(512)S(1)} %bitcast.63, f32[416,256]{1,0:T(8,128)S(1)} %concatenate.20.refs_2_), custom_call_target="tpu_custom_call" | custom-call | flops 2415919104 | bytes 4194304 | tf_op jit(solution)/shard_map/spread_own/pallas_call | solution.py:188
  20.7 2.1 %collective-permute-done.4.refs_2_.refs_3_ = f32[416,256]{1,0:T(8,128)S(1)} collective-permute-done((f32[416,256]{1,0:T(8,128)S(1)}, f32[416,256]{1,0:T(8,128)S(1)}, u32[]{:S(2)}, u32[]{:S(2)}) %collective-permute-start.4) | collective-permute-done | bytes 426016 | tf_op jit(solution)/shard_map/ppermute | solution.py:25
  23.1 0.9 collective-permute-done.6.refs_4_.refs_5_.refs_3_
  24.0 2.3 %collective-permute-start.8 = (f32[416,256]{1,0:T(8,128)S(1)}, f32[416,256]{1,0:T(8,128)S(1)}, u32[]{:S(2)}, u32[]{:S(2)}) collective-permute-start(f32[416,256]{1,0:T(8,128)S(1)} %collective-permute-done.4.refs_2_.refs_3_), channel_id=1, source_target_pairs={{0,12},{4,0},{8,4},{12,8},{1,13},{5,1},{9,5},{13,9},{2,14},{6,2},{... | collective-permute-start | bytes 1277960 | tf_op jit(solution)/shard_map/ppermute | solution.py:25
  26.3 6.3 %spread_mid.1.refs_4_ = f32[3,3,256,128]{3,2,1,0:T(8,128)S(1)} custom-call(s32[48]{0:T(128)S(1)} %copy-done.6, s32[1536]{0:T(1024)S(1)} %maximum_convert_fusion.refs_1_, f32[416,256]{1,0:T(8,128)S(1)} %collective-permute-done.4.refs_2_.refs_3_, f32[416,256]{1,0:T(8,128)S(1)} %collective-permute-done.5.refs_3_.refs_4_.refs_2_, ...), custom_call_target="tpu_custom_call" | custom-call | flops 3221225472 | bytes 4194304 | tf_op jit(solution)/shard_map/spread_mid/pallas_call | solution.py:188
  33.0 5.9 %spread_far.1 = f32[3,3,256,128]{3,2,1,0:T(8,128)S(1)} custom-call(s32[48]{0:T(128)S(1)} %copy-done.5, s32[1024]{0:T(1024)S(1)} %maximum_convert_fusion.1.refs_1_, f32[416,256]{1,0:T(8,128)S(1)} %collective-permute-done.7.refs_2_.refs_5_.refs_6_.refs_4_, f32[416,256]{1,0:T(8,128)S(1)} %collective-permute-done.8.refs_3_.refs_6_.refs_7_.refs_5_, ...), custom_call_target="tpu_custom_call" | custom-call | flops 3221225472 | bytes 4194304 | tf_op jit(solution)/shard_map/spread_far/pallas_call | solution.py:188
  39.1 1.9 %collective-permute-start.10 = (f32[3,256,128]{2,1,0:T(8,128)S(1)}, f32[3,256,128]{2,1,0:T(8,128)S(1)}, u32[]{:S(2)}, u32[]{:S(2)}) collective-permute-start(f32[3,256,128]{2,1,0:T(8,128)S(1)} %get-tuple-element.33), channel_id=1, source_target_pairs={{0,1},{1,2},{2,3},{3,0},{4,5},{5,6},{6,7},{7,4},{8,9},{9,10},{10,1... | collective-permute-start | bytes 1179656 | tf_op jit(solution)/shard_map/ppermute | solution.py:25
  41.0 2.1 %collective-permute-start.9 = (f32[3,256,128]{2,1,0:T(8,128)S(1)}, f32[3,256,128]{2,1,0:T(8,128)S(1)}, u32[]{:S(2)}, u32[]{:S(2)}) collective-permute-start(f32[3,256,128]{2,1,0:T(8,128)S(1)} %get-tuple-element.34), channel_id=1, source_target_pairs={{0,3},{1,0},{2,1},{3,2},{4,7},{5,4},{6,5},{7,6},{8,11},{9,8},{10,9... | collective-permute-start | bytes 1179656 | tf_op jit(solution)/shard_map/ppermute | solution.py:25
  43.1 6.4 %spread_late.1 = f32[1,3,256,128]{3,2,1,0:T(8,128)S(1)} custom-call(s32[48]{0:T(128)S(1)} %copy-done.4, s32[3072]{0:T(1024)S(1)} %pad_add_fusion.1.refs_1_, f32[416,256]{1,0:T(8,128)S(1)} %collective-permute-done.4.refs_2_.refs_3_, f32[416,256]{1,0:T(8,128)S(1)} %collective-permute-done.5.refs_3_.refs_4_.refs_2_, ...), custom_call_target="tpu_custom_call" | custom-call | flops 3221225472 | bytes 4194304 | tf_op jit(solution)/shard_map/spread_late/pallas_call | solution.py:188
  49.6 1.5 %collective-permute-done.10 = f32[3,256,128]{2,1,0:T(8,128)S(1)} collective-permute-done((f32[3,256,128]{2,1,0:T(8,128)S(1)}, f32[3,256,128]{2,1,0:T(8,128)S(1)}, u32[]{:S(2)}, u32[]{:S(2)}) %collective-permute-start.10) | collective-permute-done | bytes 393248 | tf_op jit(solution)/shard_map/ppermute | solution.py:25
  51.1 10.2 %collective-permute-done.9 = f32[3,256,128]{2,1,0:T(8,128)S(1)} collective-permute-done((f32[3,256,128]{2,1,0:T(8,128)S(1)}, f32[3,256,128]{2,1,0:T(8,128)S(1)}, u32[]{:S(2)}, u32[]{:S(2)}) %collective-permute-start.9) | collective-permute-done | bytes 393248 | tf_op jit(solution)/shard_map/ppermute | solution.py:25
  62.1 3.2 %collective-permute-start.12 = (f32[3,256,128]{2,1,0:T(8,128)S(1)}, f32[3,256,128]{2,1,0:T(8,128)S(1)}, u32[]{:S(2)}, u32[]{:S(2)}) collective-permute-start(f32[3,256,128]{2,1,0:T(8,128)S(1)} %fusion.refs_8_), channel_id=1, source_target_pairs={{0,3},{1,0},{2,1},{3,2},{4,7},{5,4},{6,5},{7,6},{8,11},{9,8},{10,9... | collective-permute-start | bytes 1179656 | tf_op jit(solution)/shard_map/ppermute | solution.py:25
  65.3 11.2 %sample_here.1 = (f32[192,256]{1,0:T(8,128)S(1)}, f32[192,256]{1,0:T(8,128)S(1)}, f32[192,256]{1,0:T(8,128)S(1)}, f32[192,256]{1,0:T(8,128)S(1)}, f32[192,256]{1,0:T(8,128)S(1)}, /*index=5*/f32[192,256]{1,0:T(8,128)S(1)}) custom-call(s32[72]{0:T(128)S(1)} %copy-done.3, s32[3072]{0:T(1024)S(1)} %pad_add_fusion.1.refs_1_, f32[416,256]{1,0:T(8,128)S(1)} %concatenate.20.refs_2_, ...), custom_call_target="tpu_custom_call" | custom-call | flops 4831838208 | bytes 4194304 | tf_op jit(solution)/shard_map/sample_here/pallas_call | solution.py:261
  76.5 4.8 %collective-permute-done.12.refs_4_.refs_7_ = f32[3,256,128]{2,1,0:T(8,128)S(1)} collective-permute-done((f32[3,256,128]{2,1,0:T(8,128)S(1)}, f32[3,256,128]{2,1,0:T(8,128)S(1)}, u32[]{:S(2)}, u32[]{:S(2)}) %collective-permute-start.12) | collective-permute-done | bytes 393248 | tf_op jit(solution)/shard_map/ppermute | solution.py:25
  81.3 9.5 %sample_far.1 = (f32[192,256]{1,0:T(8,128)S(1)}, f32[192,256]{1,0:T(8,128)S(1)}, f32[192,256]{1,0:T(8,128)S(1)}, f32[192,256]{1,0:T(8,128)S(1)}) custom-call(s32[72]{0:T(128)S(1)} %copy-done.2, s32[3072]{0:T(1024)S(1)} %pad_add_fusion.1.refs_1_, f32[416,256]{1,0:T(8,128)S(1)} %collective-permute-done.5.refs_3_.refs_4_.refs_2_, ...), custom_call_target="tpu_custom_call" | custom-call | flops 4831838208 | bytes 4194304 | tf_op jit(solution)/shard_map/sample_far/pallas_call | solution.py:261
  92.2 1.3 %collective-permute-start.16 = (f32[192,256]{1,0:T(8,128)S(1)}, f32[192,256]{1,0:T(8,128)S(1)}, u32[]{:S(2)}, u32[]{:S(2)}) collective-permute-start(f32[192,256]{1,0:T(8,128)S(1)} %get-tuple-element.30), channel_id=1, source_target_pairs={{0,12},{4,0},{8,4},{12,8},{1,13},{5,1},{9,5},{13,9},{2,14},{6,2},{... | collective-permute-start | bytes 589832 | tf_op jit(solution)/shard_map/ppermute | solution.py:25
  93.9 3.9 %sample_side.1 = f32[192,256]{1,0:T(8,128)S(1)} custom-call(s32[24]{0:T(128)S(1)} %copy-done.1, s32[3072]{0:T(1024)S(1)} %pad_add_fusion.1.refs_1_, f32[416,256]{1,0:T(8,128)S(1)} %collective-permute-done.4.refs_2_.refs_3_, f32[3,256,128]{2,1,0:T(8,128)S(1)} %collective-permute-done.11.refs_3_.refs_6_, ...), custom_call_target="tpu_custom_call" | custom-call | flops 1610612736 | bytes 4194304 | tf_op jit(solution)/shard_map/sample_side/pallas_call | solution.py:261
  98.4 5.0 %collective-permute-start.15 = (f32[192,256]{1,0:T(8,128)S(1)}, f32[192,256]{1,0:T(8,128)S(1)}, u32[]{:S(2)}, u32[]{:S(2)}) collective-permute-start(f32[192,256]{1,0:T(8,128)S(1)} %add_add_fusion.1), channel_id=1, source_target_pairs={{0,16},{16,0},{1,17},{17,1},{2,18},{18,2},{3,19},{19,3},{4,20},{20... | collective-permute-start | bytes 589832 | tf_op jit(solution)/shard_map/ppermute | solution.py:25
  104.2 2.3 %sample_own.1 = f32[192,256]{1,0:T(8,128)S(1)} custom-call(s32[12]{0:T(128)S(1)} %copy-done, s32[3072]{0:T(1024)S(1)} %pad_add_fusion.1.refs_1_, f32[416,256]{1,0:T(8,128)S(1)} %concatenate.20.refs_2_, f32[3,256,128]{2,1,0:T(8,128)S(1)} %collective-permute-done.11.refs_3_.refs_6_, f32[3,256,128]{2,1,0:T(8,128)S(1)} %collective-permute-done.12.refs_4_.refs_7_, ...), custom_call_target="tpu_custom_call" | custom-call | flops 805306368 | bytes 4194304 | tf_op jit(solution)/shard_map/sample_own/pallas_call | solution.py:261
  (105 shorter events, 10.1 us)
Async XLA Ops:
  0.6 8.7 %copy-start.9 = (s32[64,27,16]{0,2,1:T(8,128)S(1)}, s32[64,27,16]{0,2,1:T(8,128)}, u32[]{:S(2)}) copy-start(s32[64,27,16]{0,2,1:T(8,128)} %param.17) | copy-start | bytes 331780
  1.8 8.6 %copy-start.8 = (f32[16,16,3,128]{3,1,2,0:T(8,128)S(1)}, f32[16,16,3,128]{3,1,2,0:T(8,128)}, u32[]{:S(2)}) copy-start(f32[16,16,3,128]{3,1,2,0:T(8,128)} %param.13) | copy-start | bytes 1179652
  1.9 8.8 %collective-permute-start = (f32[3,16,128]{2,1,0:T(8,128)S(1)}, f32[3,16,128]{2,1,0:T(8,128)S(1)}, u32[]{:S(2)}, u32[]{:S(2)}) collective-permute-start(f32[3,16,128]{2,1,0:T(8,128)S(1)} %bitcast.73), channel_id=1, source_target_pairs={{0,16},{16,0},{1,17},{17,1},{2,18},{18,2},{3,19},{19,3},{4,20},{20... | collective-permute-start | bytes 73736 | tf_op jit(solution)/shard_map/ppermute | solution.py:25
  5.0 5.8 %collective-permute-start.1 = (f32[3,16,128]{2,1,0:T(8,128)S(1)}, f32[3,16,128]{2,1,0:T(8,128)S(1)}, u32[]{:S(2)}, u32[]{:S(2)}) collective-permute-start(f32[3,16,128]{2,1,0:T(8,128)S(1)} %bitcast.74), channel_id=1, source_target_pairs={{0,16},{16,0},{1,17},{17,1},{2,18},{18,2},{3,19},{19,3},{4,20},{20... | collective-permute-start | bytes 73736 | tf_op jit(solution)/shard_map/ppermute | solution.py:25
  5.0 5.7 %collective-permute-start.2 = (f32[3,16,128]{2,1,0:T(8,128)S(1)}, f32[3,16,128]{2,1,0:T(8,128)S(1)}, u32[]{:S(2)}, u32[]{:S(2)}) collective-permute-start(f32[3,16,128]{2,1,0:T(8,128)S(1)} %get-tuple-element.36), channel_id=1, source_target_pairs={{0,4},{4,8},{8,12},{12,0},{1,5},{5,9},{9,13},{13,1},{2,6},{6,10},{... | collective-permute-start | bytes 73736 | tf_op jit(solution)/shard_map/ppermute | solution.py:25
  5.0 5.7 %collective-permute-start.3 = (f32[3,16,128]{2,1,0:T(8,128)S(1)}, f32[3,16,128]{2,1,0:T(8,128)S(1)}, u32[]{:S(2)}, u32[]{:S(2)}) collective-permute-start(f32[3,16,128]{2,1,0:T(8,128)S(1)} %get-tuple-element.35), channel_id=1, source_target_pairs={{0,12},{4,0},{8,4},{12,8},{1,13},{5,1},{9,5},{13,9},{2,14},{6,2},{... | collective-permute-start | bytes 73736 | tf_op jit(solution)/shard_map/ppermute | solution.py:25
  10.7 12.1 %collective-permute-start.4 = (f32[416,256]{1,0:T(8,128)S(1)}, f32[416,256]{1,0:T(8,128)S(1)}, u32[]{:S(2)}, u32[]{:S(2)}) collective-permute-start(f32[416,256]{1,0:T(8,128)S(1)} %concatenate.20.refs_2_), channel_id=1, source_target_pairs={{0,16},{16,0},{1,17},{17,1},{2,18},{18,2},{3,19},{19,3},{4,20},{20... | collective-permute-start | bytes 1277960 | tf_op jit(solution)/shard_map/ppermute | solution.py:25
  12.7 10.3 %collective-permute-start.5 = (f32[416,256]{1,0:T(8,128)S(1)}, f32[416,256]{1,0:T(8,128)S(1)}, u32[]{:S(2)}, u32[]{:S(2)}) collective-permute-start(f32[416,256]{1,0:T(8,128)S(1)} %concatenate.20.refs_2_), channel_id=1, source_target_pairs={{0,4},{4,8},{8,12},{12,0},{1,5},{5,9},{9,13},{13,1},{2,6},{6,10},{... | collective-permute-start | bytes 1277960 | tf_op jit(solution)/shard_map/ppermute | solution.py:25
  12.8 11.2 %collective-permute-start.6 = (f32[416,256]{1,0:T(8,128)S(1)}, f32[416,256]{1,0:T(8,128)S(1)}, u32[]{:S(2)}, u32[]{:S(2)}) collective-permute-start(f32[416,256]{1,0:T(8,128)S(1)} %concatenate.20.refs_2_), channel_id=1, source_target_pairs={{0,12},{4,0},{8,4},{12,8},{1,13},{5,1},{9,5},{13,9},{2,14},{6,2},{... | collective-permute-start | bytes 1277960 | tf_op jit(solution)/shard_map/ppermute | solution.py:25
  14.8 11.4 %copy-start.6 = (s32[48]{0:T(128)S(1)}, s32[48]{0:T(128)}, u32[]{:S(2)}) copy-start(s32[48]{0:T(128)} %constant.37.clone.refs_0_) | copy-start | bytes 580
  22.8 10.0 %collective-permute-start.7 = (f32[416,256]{1,0:T(8,128)S(1)}, f32[416,256]{1,0:T(8,128)S(1)}, u32[]{:S(2)}, u32[]{:S(2)}) collective-permute-start(f32[416,256]{1,0:T(8,128)S(1)} %collective-permute-done.4.refs_2_.refs_3_), channel_id=1, source_target_pairs={{0,4},{4,8},{8,12},{12,0},{1,5},{5,9},{9,13},{13,1},{2,6},{6,10},{... | collective-permute-start | bytes 1277960 | tf_op jit(solution)/shard_map/ppermute | solution.py:25
  24.0 9.0 %collective-permute-start.8 = (f32[416,256]{1,0:T(8,128)S(1)}, f32[416,256]{1,0:T(8,128)S(1)}, u32[]{:S(2)}, u32[]{:S(2)}) collective-permute-start(f32[416,256]{1,0:T(8,128)S(1)} %collective-permute-done.4.refs_2_.refs_3_), channel_id=1, source_target_pairs={{0,12},{4,0},{8,4},{12,8},{1,13},{5,1},{9,5},{13,9},{2,14},{6,2},{... | collective-permute-start | bytes 1277960 | tf_op jit(solution)/shard_map/ppermute | solution.py:25
  39.1 12.0 %collective-permute-start.10 = (f32[3,256,128]{2,1,0:T(8,128)S(1)}, f32[3,256,128]{2,1,0:T(8,128)S(1)}, u32[]{:S(2)}, u32[]{:S(2)}) collective-permute-start(f32[3,256,128]{2,1,0:T(8,128)S(1)} %get-tuple-element.33), channel_id=1, source_target_pairs={{0,1},{1,2},{2,3},{3,0},{4,5},{5,6},{6,7},{7,4},{8,9},{9,10},{10,1... | collective-permute-start | bytes 1179656 | tf_op jit(solution)/shard_map/ppermute | solution.py:25
  41.0 20.3 %collective-permute-start.9 = (f32[3,256,128]{2,1,0:T(8,128)S(1)}, f32[3,256,128]{2,1,0:T(8,128)S(1)}, u32[]{:S(2)}, u32[]{:S(2)}) collective-permute-start(f32[3,256,128]{2,1,0:T(8,128)S(1)} %get-tuple-element.34), channel_id=1, source_target_pairs={{0,3},{1,0},{2,1},{3,2},{4,7},{5,4},{6,5},{7,6},{8,11},{9,8},{10,9... | collective-permute-start | bytes 1179656 | tf_op jit(solution)/shard_map/ppermute | solution.py:25
  49.6 15.7 %copy-start.3 = (s32[72]{0:T(128)S(1)}, s32[72]{0:T(128)}, u32[]{:S(2)}) copy-start(s32[72]{0:T(128)} %constant.40.clone.refs_0_) | copy-start | bytes 868
  61.4 19.9 %copy-start.2 = (s32[72]{0:T(128)S(1)}, s32[72]{0:T(128)}, u32[]{:S(2)}) copy-start(s32[72]{0:T(128)} %constant.41.clone.refs_0_) | copy-start | bytes 868
  61.4 15.1 %collective-permute-start.11 = (f32[3,256,128]{2,1,0:T(8,128)S(1)}, f32[3,256,128]{2,1,0:T(8,128)S(1)}, u32[]{:S(2)}, u32[]{:S(2)}) collective-permute-start(f32[3,256,128]{2,1,0:T(8,128)S(1)} %fusion.refs_8_), channel_id=1, source_target_pairs={{0,1},{1,2},{2,3},{3,0},{4,5},{5,6},{6,7},{7,4},{8,9},{9,10},{10,1... | collective-permute-start | bytes 1179656 | tf_op jit(solution)/shard_map/ppermute | solution.py:25
  62.1 19.3 %collective-permute-start.12 = (f32[3,256,128]{2,1,0:T(8,128)S(1)}, f32[3,256,128]{2,1,0:T(8,128)S(1)}, u32[]{:S(2)}, u32[]{:S(2)}) collective-permute-start(f32[3,256,128]{2,1,0:T(8,128)S(1)} %fusion.refs_8_), channel_id=1, source_target_pairs={{0,3},{1,0},{2,1},{3,2},{4,7},{5,4},{6,5},{7,6},{8,11},{9,8},{10,9... | collective-permute-start | bytes 1179656 | tf_op jit(solution)/shard_map/ppermute | solution.py:25
  81.3 12.5 %copy-start.1 = (s32[24]{0:T(128)S(1)}, s32[24]{0:T(128)}, u32[]{:S(2)}) copy-start(s32[24]{0:T(128)} %constant.42.clone.refs_0_) | copy-start | bytes 292
  90.8 7.0 %collective-permute-start.13 = (f32[192,256]{1,0:T(8,128)S(1)}, f32[192,256]{1,0:T(8,128)S(1)}, u32[]{:S(2)}, u32[]{:S(2)}) collective-permute-start(f32[192,256]{1,0:T(8,128)S(1)} %get-tuple-element.28), channel_id=1, source_target_pairs={{0,12},{4,0},{8,4},{12,8},{1,13},{5,1},{9,5},{13,9},{2,14},{6,2},{... | collective-permute-start | bytes 589832 | tf_op jit(solution)/shard_map/ppermute | solution.py:25
  91.7 6.6 %collective-permute-start.14 = (f32[192,256]{1,0:T(8,128)S(1)}, f32[192,256]{1,0:T(8,128)S(1)}, u32[]{:S(2)}, u32[]{:S(2)}) collective-permute-start(f32[192,256]{1,0:T(8,128)S(1)} %get-tuple-element.29), channel_id=1, source_target_pairs={{0,4},{4,8},{8,12},{12,0},{1,5},{5,9},{9,13},{13,1},{2,6},{6,10},{... | collective-permute-start | bytes 589832 | tf_op jit(solution)/shard_map/ppermute | solution.py:25
  92.2 14.3 %collective-permute-start.16 = (f32[192,256]{1,0:T(8,128)S(1)}, f32[192,256]{1,0:T(8,128)S(1)}, u32[]{:S(2)}, u32[]{:S(2)}) collective-permute-start(f32[192,256]{1,0:T(8,128)S(1)} %get-tuple-element.30), channel_id=1, source_target_pairs={{0,12},{4,0},{8,4},{12,8},{1,13},{5,1},{9,5},{13,9},{2,14},{6,2},{... | collective-permute-start | bytes 589832 | tf_op jit(solution)/shard_map/ppermute | solution.py:25
  93.5 13.0 %collective-permute-start.17 = (f32[192,256]{1,0:T(8,128)S(1)}, f32[192,256]{1,0:T(8,128)S(1)}, u32[]{:S(2)}, u32[]{:S(2)}) collective-permute-start(f32[192,256]{1,0:T(8,128)S(1)} %get-tuple-element.31), channel_id=1, source_target_pairs={{0,4},{4,8},{8,12},{12,0},{1,5},{5,9},{9,13},{13,1},{2,6},{6,10},{... | collective-permute-start | bytes 589832 | tf_op jit(solution)/shard_map/ppermute | solution.py:25
  98.4 8.6 %collective-permute-start.15 = (f32[192,256]{1,0:T(8,128)S(1)}, f32[192,256]{1,0:T(8,128)S(1)}, u32[]{:S(2)}, u32[]{:S(2)}) collective-permute-start(f32[192,256]{1,0:T(8,128)S(1)} %add_add_fusion.1), channel_id=1, source_target_pairs={{0,16},{16,0},{1,17},{17,1},{2,18},{18,2},{3,19},{19,3},{4,20},{20... | collective-permute-start | bytes 589832 | tf_op jit(solution)/shard_map/ppermute | solution.py:25
  (7 other events, 33.0 us)
